TPU v7x, 32 devices: a whole 2x2x4 slice. The times are simulated.
32 devices in a mesh: grp: 2 (over y), ctx: 4 (over z), hd: 4 (over x, core).
Axes of the slice: x: 2, y: 2, z: 4, core: 2. Of those that a mesh axis runs over, the one named last changes fastest.
Arguments:
- query: bfloat16 [1024, 4096], P(('grp', 'ctx'), 'hd'), parts along dimension 0, may hold values from -6 to 6
- keys: bfloat16 [1024, 1024], P(('grp', 'ctx'), 'hd'), parts along dimension 0, may hold values from -6 to 6
- values: bfloat16 [1024, 1024], P(('grp', 'ctx'), 'hd'), parts along dimension 0, may hold values from -6 to 6
- m_x: bfloat16 [1024, 8192], P(('grp', 'ctx'), 'hd'), parts along dimension 0, may hold values from -6 to 6
- m_z: bfloat16 [1024, 8192], P(('grp', 'ctx'), 'hd'), parts along dimension 0, may hold values from -6 to 6
- m_b: bfloat16 [1024, 1024], P(('grp', 'ctx'), 'hd'), parts along dimension 0, may hold values from -6 to 6
- m_c: bfloat16 [1024, 1024], P(('grp', 'ctx'), 'hd'), parts along dimension 0, may hold values from -0.5 to 0.5
- dt_raw: bfloat16 [1024, 128], P(('grp', 'ctx'), 'hd'), parts along dimension 0, may hold values from -5 to 25
- dt_bias: float32 [128], P('hd'), may hold values from -0.5 to 0.5
- a_log: float32 [128], P('hd'), may hold values from -10 to 0
- d_skip: float32 [128], P('hd'), may hold values from 0.5 to 2
- norm_gain: float32 [8192], P('hd'), may hold values from 0.5 to 1.5
Outputs:
- context: bfloat16 [1024, 4096], P(('grp', 'ctx'), 'hd'), parts along dimension 0
- mixed: bfloat16 [1024, 8192], P(('grp', 'ctx'), 'hd'), parts along dimension 0
There are 2 independent parts, one for each index of `grp`. A program takes and returns all parts, laid end to end along the dimension named above; an argument that names none is the same for every part. Nothing has to cross between parts.
All inputs are finite; a program needn't handle non-finite values.
Results may differ from a plain program's by a relative error of at most 0.009.
Values may be sent and summed in bfloat16 or wider, within the bound.
A program may use at most 64 MiB of HBM per device.

v0:
```python
import math
import jax
import jax.numpy as jnp
from jax import lax
from jax.sharding import PartitionSpec as P

HEAD_SIZE = 128
MP = 64
MN = 128
highest = lax.Precision.HIGHEST
norm_eps = 1e-05
masked_score = -1e30


def token_position(row_index, tok_rows, ctx_count):
    device = row_index // tok_rows
    within = row_index - device * tok_rows
    half_rows = tok_rows // 2
    second = within >= half_rows
    block_index = jnp.where(second, 2 * ctx_count - 1 - device, device)
    return block_index * half_rows + within - jnp.where(second, half_rows, 0)


def pick_block(total_rows, limit):
    selected = 1
    for candidate in range(1, min(total_rows, limit) + 1):
        if total_rows % candidate == 0:
            selected = candidate
    return selected


def folded_to_sequence(whole, ctx_count):
    half_rows = whole.shape[0] // (2 * ctx_count)
    blocks = whole.reshape((ctx_count, 2, half_rows) + whole.shape[1:])
    return jnp.concatenate([blocks[:, 0], blocks[::-1, 1]], axis=0).reshape(whole.shape)


def attend(query, keys, values):
    tok_rows = query.shape[0]
    ctx_count = lax.axis_size("ctx")
    kv_local = keys.shape[1] // HEAD_SIZE
    heads_per_group = query.shape[1] // keys.shape[1]
    query_heads = query.reshape(tok_rows, kv_local, heads_per_group, HEAD_SIZE)
    own_rows = lax.axis_index("ctx") * tok_rows + jnp.arange(tok_rows, dtype=jnp.int32)
    query_pos = token_position(own_rows, tok_rows, ctx_count)
    scaling = 1.0 / math.sqrt(HEAD_SIZE)
    start_max = jnp.full((kv_local, heads_per_group, tok_rows), masked_score, jnp.float32)
    start_sum = jnp.zeros((kv_local, heads_per_group, tok_rows), jnp.float32)
    start_acc = jnp.zeros((kv_local, heads_per_group, tok_rows, HEAD_SIZE), jnp.float32)
    start = jnp.int32(0)
    key_piece = lax.all_gather(keys, "ctx", axis=0, tiled=True)
    value_piece = lax.all_gather(values, "ctx", axis=0, tiled=True)
    piece_rows = key_piece.shape[0]
    rows_per_block = pick_block(piece_rows, 1024)

    def one_block(index, running):
        running_max, running_sum, running_acc = running
        offset = index * rows_per_block
        key_block = lax.dynamic_slice_in_dim(key_piece, offset, rows_per_block, 0).reshape(
            rows_per_block, kv_local, HEAD_SIZE
        )
        value_block = lax.dynamic_slice_in_dim(value_piece, offset, rows_per_block, 0).reshape(
            rows_per_block, kv_local, HEAD_SIZE
        )
        key_pos = token_position(
            start + offset + jnp.arange(rows_per_block, dtype=jnp.int32), tok_rows, ctx_count
        )
        visible = key_pos[None, :] <= query_pos[:, None]
        scores = (
            jnp.einsum("qhgd,khd->hgqk", query_heads, key_block, preferred_element_type=jnp.float32)
            * scaling
        )
        scores = jnp.where(visible, scores, masked_score)
        new_max = jnp.maximum(running_max, jnp.max(scores, axis=-1))
        weights = jnp.where(visible, jnp.exp(scores - new_max[..., None]), 0.0)
        factor = jnp.exp(running_max - new_max)
        new_sum = running_sum * factor + jnp.sum(weights, axis=-1)
        update = jnp.einsum(
            "hgqk,khd->hgqd",
            weights.astype(jnp.bfloat16),
            value_block,
            preferred_element_type=jnp.float32,
        )
        return (new_max, new_sum, running_acc * factor[..., None] + update)

    final_max, final_sum, final_acc = lax.fori_loop(
        0, piece_rows // rows_per_block, one_block, (start_max, start_sum, start_acc)
    )
    averaged = final_acc / final_sum[..., None]
    return jnp.transpose(averaged, (2, 0, 1, 3)).reshape(tok_rows, -1).astype(jnp.bfloat16)


def ssd_block(inputs, steps, rates, b_rows, c_rows):
    intersection = jnp.dot(c_rows, b_rows.T, preferred_element_type=jnp.float32)
    inputs = inputs.astype(jnp.float32)
    b_rows = b_rows.astype(jnp.float32)
    sequence_length = inputs.shape[0]
    running = jnp.cumsum(-steps * rates, axis=0)
    lower = jnp.arange(sequence_length)[:, None] >= jnp.arange(sequence_length)[None, :]
    spread = running[:, None, :] - running[None, :, :]
    decay = jnp.exp(jnp.where(lower[:, :, None], spread, -jnp.inf))
    weights = intersection[:, :, None] * decay * steps[None, :, :]
    inner = jnp.einsum("ijh,jhp->ihp", weights, inputs, precision=highest)
    tail_weight = jnp.exp(running[-1][None, :] - running) * steps
    state = jnp.einsum("jh,jhp,jn->hpn", tail_weight, inputs, b_rows, precision=highest)
    return (inner, state, jnp.exp(running[-1]), jnp.exp(running))


def chain_states(earlier, later):
    return (earlier[0] * later[0], earlier[1] * later[0][..., None, None] + later[1])


def ssd_sequence(inputs, steps, rates, b_rows, c_rows):
    sequence_length, head_count, width = inputs.shape
    block_len = math.gcd(sequence_length, 128)
    count = sequence_length // block_len
    c_blocks = c_rows.reshape(count, block_len, -1)
    inner, state, totals, scaled = jax.vmap(ssd_block, in_axes=(0, 0, None, 0, 0))(
        inputs.reshape(count, block_len, head_count, width),
        steps.reshape(count, block_len, head_count),
        rates,
        b_rows.reshape(count, block_len, -1),
        c_blocks,
    )
    running = lax.associative_scan(chain_states, (totals, state))
    entering = jnp.concatenate([jnp.zeros_like(running[1][:1]), running[1][:-1]], axis=0)
    carried = (
        jnp.einsum("cqn,chpn->cqhp", c_blocks.astype(jnp.float32), entering, precision=highest)
        * scaled[..., None]
    )
    return (inner + carried).reshape(sequence_length, head_count, width)


def gated_norm(gated_rows, norm_scale, group_count):
    row_count = gated_rows.shape[0]
    widened = (
        lax.optimization_barrier(gated_rows).astype(jnp.float32).reshape(row_count, group_count, -1)
    )
    power = jnp.mean(widened * widened, axis=-1, keepdims=True)
    return ((widened * lax.rsqrt(power + norm_eps)).reshape(row_count, -1) * norm_scale).astype(
        jnp.bfloat16
    )


def body(query, keys, values, m_x, m_z, m_b, m_c, dt_raw, dt_bias, a_log, d_skip, norm_gain):
    ctx_count = lax.axis_size("ctx")
    context_fold = attend(query, keys, values)
    heads_here = dt_bias.shape[0]
    groups_here = m_b.shape[1] // MN
    per_group = heads_here // groups_here
    rates = jnp.exp(a_log)
    x_cols, z_cols, context_cols = (
        lax.all_to_all(m_x, "ctx", split_axis=1, concat_axis=0, tiled=True),
        lax.all_to_all(m_z, "ctx", split_axis=1, concat_axis=0, tiled=True),
        lax.all_to_all(context_fold, "ctx", split_axis=1, concat_axis=0, tiled=True),
    )
    dt_whole, b_whole, c_whole = (
        lax.all_gather(dt_raw, "ctx", axis=0, tiled=True),
        lax.all_gather(m_b, "ctx", axis=0, tiled=True),
        lax.all_gather(m_c, "ctx", axis=0, tiled=True),
    )
    x_cols = folded_to_sequence(x_cols, ctx_count)
    z_cols = folded_to_sequence(z_cols, ctx_count)
    context_cols = folded_to_sequence(context_cols, ctx_count)
    dt_whole = folded_to_sequence(dt_whole, ctx_count)
    b_whole = folded_to_sequence(b_whole, ctx_count)
    c_whole = folded_to_sequence(c_whole, ctx_count)
    sequence_length = x_cols.shape[0]
    width = x_cols.shape[1]
    sub_width = min(width, MP)
    head_count = width // sub_width
    first_head = lax.axis_index("ctx") * width // MP
    group_index = first_head // per_group
    step_mine = jax.nn.softplus(
        lax.dynamic_slice_in_dim(dt_whole, first_head, head_count, 1).astype(jnp.float32)
        + lax.dynamic_slice_in_dim(dt_bias, first_head, head_count, 0)
    )
    rate_mine = lax.dynamic_slice_in_dim(rates, first_head, head_count, 0)
    skip_mine = lax.dynamic_slice_in_dim(d_skip, first_head, head_count, 0)
    b_mine = lax.dynamic_slice_in_dim(b_whole, group_index * MN, MN, 1)
    c_mine = lax.dynamic_slice_in_dim(c_whole, group_index * MN, MN, 1)
    x_mine = x_cols.reshape(sequence_length, head_count, sub_width)
    outputs = ssd_sequence(x_mine, step_mine, rate_mine, b_mine, c_mine)
    outputs = outputs + skip_mine[None, :, None] * x_mine.astype(jnp.float32)
    gated = (
        outputs.reshape(sequence_length, width) * jax.nn.silu(z_cols.astype(jnp.float32))
    ).astype(jnp.bfloat16)
    gated_rows, context = (
        lax.all_to_all(gated, "ctx", split_axis=0, concat_axis=1, tiled=True),
        lax.all_to_all(context_cols, "ctx", split_axis=0, concat_axis=1, tiled=True),
    )
    mixed = gated_norm(gated_rows, norm_gain, groups_here)
    return (context, mixed)


def solution(mesh):
    in_specs = (
        P(("grp", "ctx"), "hd"),
        P(("grp", "ctx"), "hd"),
        P(("grp", "ctx"), "hd"),
        P(("grp", "ctx"), "hd"),
        P(("grp", "ctx"), "hd"),
        P(("grp", "ctx"), "hd"),
        P(("grp", "ctx"), "hd"),
        P(("grp", "ctx"), "hd"),
        P("hd"),
        P("hd"),
        P("hd"),
        P("hd"),
    )
    out_specs = (P(("grp", "ctx"), "hd"), P(("grp", "ctx"), "hd"))
    return jax.shard_map(body, mesh=mesh, in_specs=in_specs, out_specs=out_specs, check_vma=False)
```

profile of v0, /device:TPU:0, one launch (start us, length us, event | category | flops | bytes accessed | tf_op | source)
XLA Modules:
  0.0 158.5 jit_solution(12240753231804312375)
XLA Ops:
  0.6 15.9 %all_gather.16 = bf16[512,256]{1,0:T(8,128)(2,1)S(1)} all-gather(bf16[128,256]{1,0:T(8,128)(2,1)} %param.14), channel_id=1, replica_groups=mesh['grp'=2,'ctx'=4,'hd'=4] {'ctx'}, dimensions={0}, use_global_device_ids=true | all-gather | bytes 327680 | tf_op jit(solution)/shard_map/all_gather | solution.py:52
  16.5 0.1 copy.70
  16.7 1.0 copy.67
  17.6 13.3 %all_gather.15 = bf16[512,256]{0,1:T(8,128)(2,1)S(1)} all-gather(bf16[128,256]{0,1:T(8,128)(2,1)S(1)} %copy.67), channel_id=1, replica_groups=mesh['grp'=2,'ctx'=4,'hd'=4] {'ctx'}, dimensions={0}, use_global_device_ids=true | all-gather | bytes 327680 | tf_op jit(solution)/shard_map/all_gather | solution.py:51
  30.9 1.1 reshape.189
  32.0 0.1 broadcast_compare_fusion
  32.2 0.5 fusion.8
  32.8 0.5 fusion.9
  33.3 0.7 fusion.17
  34.0 0.9 copy.72
  34.9 4.2 %all-to-all-start = ((bf16[128,4,256]{2,0,1:T(8,128)(2,1)}), bf16[128,4,256]{2,0,1:T(8,128)(2,1)S(1)}, u32[]{:S(2)}, u32[]{:S(2)}) async-start(bf16[128,4,256]{2,0,1:T(8,128)(2,1)} %copy.72), calls=%async_computation | async-start | bytes 524288 | tf_op jit(solution)/shard_map/all_to_all | solution.py:155
  39.0 13.6 %all_gather.19 = bf16[512,32]{0,1:T(8,128)(2,1)S(1)} all-gather(bf16[128,32]{0,1:T(8,128)(2,1)S(1)} %copy-done.10), channel_id=1, replica_groups=mesh['grp'=2,'ctx'=4,'hd'=4] {'ctx'}, dimensions={0}, use_global_device_ids=true | all-gather | bytes 40960 | tf_op jit(solution)/shard_map/all_gather | solution.py:158
  52.7 0.1 reshape.199
  52.8 0.1 fusion.60
  53.1 0.1 reshape.200
  53.2 0.1 dynamic_slice.25
  53.3 0.1 compare_select_fusion
  53.4 0.1 copy.82
  53.5 0.1 dynamic_slice.26
  53.6 14.5 %all_gather.18 = bf16[512,256]{1,0:T(8,128)(2,1)S(1)} all-gather(bf16[128,256]{1,0:T(8,128)(2,1)S(1)} %copy-done.4), channel_id=1, replica_groups=mesh['grp'=2,'ctx'=4,'hd'=4] {'ctx'}, dimensions={0}, use_global_device_ids=true | all-gather | bytes 327680 | tf_op jit(solution)/shard_map/all_gather | solution.py:159
  68.1 14.5 %all_gather.17 = bf16[512,256]{1,0:T(8,128)(2,1)S(1)} all-gather(bf16[128,256]{1,0:T(8,128)(2,1)S(1)} %copy-done.5), channel_id=1, replica_groups=mesh['grp'=2,'ctx'=4,'hd'=4] {'ctx'}, dimensions={0}, use_global_device_ids=true | all-gather | bytes 327680 | tf_op jit(solution)/shard_map/all_gather | solution.py:160
  82.7 0.3 reduce_window_sum.11
  83.0 0.1 fusion.59
  83.1 0.7 copy.85
  83.8 0.7 copy.83
  84.6 1.0 copy.74
  85.6 1.0 copy.90
  86.6 0.1 copy.88
  86.7 0.1 dynamic_slice.27
  86.9 0.7 mul.219
  87.6 3.5 %all-to-all-start.2 = ((bf16[128,4,512]{0,2,1:T(8,128)(2,1)}), bf16[128,4,512]{0,2,1:T(8,128)(2,1)S(1)}, u32[]{:S(2)}, u32[]{:S(2)}) async-start(bf16[128,4,512]{0,2,1:T(8,128)(2,1)} %bitcast.18), calls=%async_computation.2 | async-start | bytes 1048576 | tf_op jit(solution)/shard_map/all_to_all | solution.py:153
  91.1 0.6 iota_compare_fusion
  91.8 0.9 fusion.61
  92.7 11.7 %all-to-all-done.2 = bf16[128,4,512]{0,2,1:T(8,128)(2,1)S(1)} async-done(((bf16[128,4,512]{0,2,1:T(8,128)(2,1)}), bf16[128,4,512]{0,2,1:T(8,128)(2,1)S(1)}, u32[]{:S(2)}, u32[]{:S(2)}) %all-to-all-start.2) | async-done | bytes 524320 | tf_op jit(solution)/shard_map/all_to_all | solution.py:153
  104.4 3.5 %all-to-all-start.3 = ((bf16[128,4,512]{0,2,1:T(8,128)(2,1)}), bf16[128,4,512]{0,2,1:T(8,128)(2,1)S(1)}, u32[]{:S(2)}, u32[]{:S(2)}) async-start(bf16[128,4,512]{0,2,1:T(8,128)(2,1)} %bitcast.46), calls=%async_computation.3 | async-start | bytes 1048576 | tf_op jit(solution)/shard_map/all_to_all | solution.py:154
  107.9 0.7 pad_maximum_fusion.3
  108.6 0.2 copy.75
  108.9 10.5 %all-to-all-done.3 = bf16[128,4,512]{0,2,1:T(8,128)(2,1)S(1)} async-done(((bf16[128,4,512]{0,2,1:T(8,128)(2,1)}), bf16[128,4,512]{0,2,1:T(8,128)(2,1)S(1)}, u32[]{:S(2)}, u32[]{:S(2)}) %all-to-all-start.3) | async-done | bytes 524320 | tf_op jit(solution)/shard_map/all_to_all | solution.py:154
  119.5 4.2 %all-to-all-start.1 = ((bf16[4,128,256]{2,1,0:T(8,128)(2,1)}), bf16[4,128,256]{2,1,0:T(8,128)(2,1)}, u32[]{:S(2)}, u32[]{:S(2)}) async-start(bf16[4,128,256]{2,1,0:T(8,128)(2,1)} %bitcast.15), calls=%async_computation.1 | async-start | bytes 524288 | tf_op jit(solution)/shard_map/all_to_all | solution.py:190
  123.7 0.2 copy.91
  124.0 0.9 pad_maximum_fusion
  124.9 0.5 reshape_reshape_reshape.3
  125.4 0.6 convert_multiply_fusion
  126.1 1.8 %fusion = f32[4,8,64,128]{3,2,1,0:T(8,128)S(1)} fusion(bf16[4,128,128,1]{2,1,3,0:T(8,128)(2,1)S(1)} %bitcast.143, f32[4,128,8,64]{3,2,1,0:T(8,128)S(1)} %convert_multiply_fusion), kind=kOutput, calls=%fused_computation.1 | convolution fusion | flops 402653184 | bytes 2228224 | tf_op jit(solution)/shard_map/vmap(jh,jhp,jn->hpn)/dot_general | solution.py:105
  127.9 0.1 slice_add_fusion
  128.0 0.1 fusion.58
  128.1 0.9 pad_add_fusion
  128.9 0.1 fusion.57
  129.1 0.2 pad.33
  129.3 6.2 %pad.61 = f32[4,8,64,128]{3,2,1,0:T(8,128)S(1)} pad(f32[2,8,64,128]{3,2,1,0:T(8,128)} %pad_add_fusion, f32[]{:T(128)} %constant.92.clone.1), padding=1_0_1x0_0_0x0_0_0x0_0_0 | pad | bytes 1572868
  135.5 0.1 slice_add_fusion.2
  135.6 0.8 copy-done.3
  136.5 2.7 %fusion.11 = f32[4,128,8,64]{1,3,2,0:T(8,128)S(1)} fusion(bf16[4,128,8,64]{3,2,1,0:T(8,128)(2,1)S(1)} %reshape_reshape_reshape.3, f32[4,128,8]{1,2,0:T(8,128)S(1)} %copy-done.6, f32[4,128,8]{1,2,0:T(8,128)S(1)} %copy-done.7, f32[4,128,128]{2,1,0:T(8,128)S(1)} %copy-done.3, pred[128,128]{1,0:T(8,128)(4,1)S(1)} %copy-done.8), kind=kOutput, calls=%fused_computation.14 | convolution fusion | flops 404750336 | bytes 1884160 | tf_op jit(solution)/shard_map/vmap(ijh,jhp->ihp)/dot_general | solution.py:103
  139.2 0.6 fusion.14
  139.8 0.3 copy.89
  140.2 1.2 fusion.36
  141.4 5.0 %all-to-all-start.4 = ((bf16[4,128,512]{2,1,0:T(8,128)(2,1)}), bf16[4,128,512]{2,1,0:T(8,128)(2,1)S(1)}, u32[]{:S(2)}, u32[]{:S(2)}) async-start(bf16[4,128,512]{2,1,0:T(8,128)(2,1)} %fusion.36), calls=%async_computation.4 | async-start | bytes 1048576 | tf_op jit(solution)/shard_map/all_to_all | solution.py:189
  146.4 1.1 copy.73
  147.5 0.9 copy.94
  148.4 8.3 %all-to-all-done.4 = bf16[4,128,512]{2,1,0:T(8,128)(2,1)S(1)} async-done(((bf16[4,128,512]{2,1,0:T(8,128)(2,1)}), bf16[4,128,512]{2,1,0:T(8,128)(2,1)S(1)}, u32[]{:S(2)}, u32[]{:S(2)}) %all-to-all-start.4) | async-done | bytes 524320 | tf_op jit(solution)/shard_map/all_to_all | solution.py:189
  156.7 0.3 copy.93
  156.9 0.2 bitcast_reduce_fusion
  157.1 0.3 fusion.19
  157.5 1.0 copy.95
  (64 shorter events, 0.8 us)
Async XLA Ops:
  33.3 5.7 %copy-start.10 = (bf16[128,32]{0,1:T(8,128)(2,1)S(1)}, bf16[128,32]{0,1:T(8,128)(2,1)}, u32[]{:S(2)}) copy-start(bf16[128,32]{0,1:T(8,128)(2,1)} %param.19) | copy-start | bytes 24580
  34.0 19.2 %copy-start.12 = (f32[32]{0:T(128)S(1)}, f32[32]{0:T(128)}, u32[]{:S(2)}) copy-start(f32[32]{0:T(128)} %param.20) | copy-start | bytes 388
  34.0 19.5 %copy-start.13 = (f32[32]{0:T(128)S(1)}, f32[32]{0:T(128)}, u32[]{:S(2)}) copy-start(f32[32]{0:T(128)} %param.21) | copy-start | bytes 388
  34.0 19.6 %copy-start.4 = (bf16[128,256]{1,0:T(8,128)(2,1)S(1)}, bf16[128,256]{1,0:T(8,128)(2,1)}, u32[]{:S(2)}) copy-start(bf16[128,256]{1,0:T(8,128)(2,1)} %param.17) | copy-start | bytes 196612
  34.0 34.1 %copy-start.5 = (bf16[128,256]{1,0:T(8,128)(2,1)S(1)}, bf16[128,256]{1,0:T(8,128)(2,1)}, u32[]{:S(2)}) copy-start(bf16[128,256]{1,0:T(8,128)(2,1)} %param.18) | copy-start | bytes 196612
  34.9 52.8 %all-to-all-start = ((bf16[128,4,256]{2,0,1:T(8,128)(2,1)}), bf16[128,4,256]{2,0,1:T(8,128)(2,1)S(1)}, u32[]{:S(2)}, u32[]{:S(2)}) async-start(bf16[128,4,256]{2,0,1:T(8,128)(2,1)} %copy.72), calls=%async_computation | async-start | bytes 524288 | tf_op jit(solution)/shard_map/all_to_all | solution.py:155
  68.1 16.5 %copy-start.1 = (bf16[128,2048]{1,0:T(8,128)(2,1)S(1)}, bf16[128,2048]{1,0:T(8,128)(2,1)}, u32[]{:S(2)}) copy-start(bf16[128,2048]{1,0:T(8,128)(2,1)} %param.15) | copy-start | bytes 1572868
  82.7 2.9 %copy-start.2 = (bf16[128,2048]{1,0:T(8,128)(2,1)S(1)}, bf16[128,2048]{1,0:T(8,128)(2,1)}, u32[]{:S(2)}) copy-start(bf16[128,2048]{1,0:T(8,128)(2,1)} %param.16) | copy-start | bytes 1572868
  83.0 3.7 %copy-start.14 = (f32[32]{0:T(128)S(1)}, f32[32]{0:T(128)}, u32[]{:S(2)}) copy-start(f32[32]{0:T(128)} %param.22) | copy-start | bytes 388
  87.6 16.7 %all-to-all-start.2 = ((bf16[128,4,512]{0,2,1:T(8,128)(2,1)}), bf16[128,4,512]{0,2,1:T(8,128)(2,1)S(1)}, u32[]{:S(2)}, u32[]{:S(2)}) async-start(bf16[128,4,512]{0,2,1:T(8,128)(2,1)} %bitcast.18), calls=%async_computation.2 | async-start | bytes 1048576 | tf_op jit(solution)/shard_map/all_to_all | solution.py:153
  104.4 15.1 %all-to-all-start.3 = ((bf16[128,4,512]{0,2,1:T(8,128)(2,1)}), bf16[128,4,512]{0,2,1:T(8,128)(2,1)S(1)}, u32[]{:S(2)}, u32[]{:S(2)}) async-start(bf16[128,4,512]{0,2,1:T(8,128)(2,1)} %bitcast.46), calls=%async_computation.3 | async-start | bytes 1048576 | tf_op jit(solution)/shard_map/all_to_all | solution.py:154
  119.5 21.9 %all-to-all-start.1 = ((bf16[4,128,256]{2,1,0:T(8,128)(2,1)}), bf16[4,128,256]{2,1,0:T(8,128)(2,1)}, u32[]{:S(2)}, u32[]{:S(2)}) async-start(bf16[4,128,256]{2,1,0:T(8,128)(2,1)} %bitcast.15), calls=%async_computation.1 | async-start | bytes 524288 | tf_op jit(solution)/shard_map/all_to_all | solution.py:190
  135.5 0.9 copy-start.3
  135.5 1.0 copy-start.6
  135.5 1.0 copy-start.7
  135.5 0.9 copy-start.8
  139.2 1.0 copy-start
  139.2 1.0 copy-start.11
  141.4 15.7 %copy-start.9 = (f32[2048]{0:T(1024)S(1)}, f32[2048]{0:T(1024)}, u32[]{:S(2)}) copy-start(f32[2048]{0:T(1024)} %param.23) | copy-start | bytes 24580
  141.4 15.3 %all-to-all-start.4 = ((bf16[4,128,512]{2,1,0:T(8,128)(2,1)}), bf16[4,128,512]{2,1,0:T(8,128)(2,1)S(1)}, u32[]{:S(2)}, u32[]{:S(2)}) async-start(bf16[4,128,512]{2,1,0:T(8,128)(2,1)} %fusion.36), calls=%async_computation.4 | async-start | bytes 1048576 | tf_op jit(solution)/shard_map/all_to_all | solution.py:189
where the time goes:
time: 160 us; the launch traced here: 158 us
  blocking collectives  71.8 us (45%)
  waiting for transfers between devices  30.6 us (19%)
  local copies, waits for them, and re-layouts  20.3 us (13%)
  starting transfers between devices  20.3 us (13%)
  matrix products  7.27 us (5%)
  other arithmetic  7.03 us (4%)
    all_gather x1, blocking collectives, attend(): value_piece = lax.all_gather(values, 'ctx', axis=0, tiled=True)  15.9 us
    all_gather x1, blocking collectives, body(): lax.all_gather(m_c, 'ctx', axis=0, tiled=True)  14.5 us
    all_gather x1, blocking collectives, body(): lax.all_gather(m_b, 'ctx', axis=0, tiled=True)  14.5 us
    all_gather x1, blocking collectives, body(): lax.all_gather(dt_raw, 'ctx', axis=0, tiled=True)  13.6 us
    all_gather x1, blocking collectives, attend(): key_piece = lax.all_gather(keys, 'ctx', axis=0, tiled=True)  13.3 us
    unnamed x36, local copies, waits for them, and re-layouts  12 us
    all_to_all x1, waiting for transfers between devices, body(): lax.all_to_all(m_x, 'ctx', split_axis=1, concat_axis=0, tiled=True)  11.7 us
    all_to_all x1, waiting for transfers between devices, body(): lax.all_to_all(m_z, 'ctx', split_axis=1, concat_axis=0, tiled=True)  10.5 us
  transfers between devices with their start and end apart: 5, of which 3 were waited for; matrix products, arithmetic and copies ran while one was open for 17% of the time, Pallas kernels for 0%

commit v1 on v0

--- a/solution.py
+++ b/solution.py
@@ -10,6 +10,13 @@
 highest = lax.Precision.HIGHEST
 norm_eps = 1e-05
 masked_score = -1e30
+
+
+def _shape_lots_all(u_in, in_array, ax_name):
+    part_next = jnp.concatenate([u_in, in_array], 1)
+    outer = lax.all_gather(part_next, ax_name, axis=0, tiled=True)
+    response = jnp.split(outer, [u_in.shape[1]], 1)
+    return response
 
 
 def token_position(row_index, tok_rows, ctx_count):
@@ -48,8 +55,7 @@
     start_sum = jnp.zeros((kv_local, heads_per_group, tok_rows), jnp.float32)
     start_acc = jnp.zeros((kv_local, heads_per_group, tok_rows, HEAD_SIZE), jnp.float32)
     start = jnp.int32(0)
-    key_piece = lax.all_gather(keys, "ctx", axis=0, tiled=True)
-    value_piece = lax.all_gather(values, "ctx", axis=0, tiled=True)
+    key_piece, value_piece = _shape_lots_all(keys, values, "ctx")
     piece_rows = key_piece.shape[0]
     rows_per_block = pick_block(piece_rows, 1024)
 

time: 160 us -> 149 us (0.931)
  blocking collectives: 71.8 us -> 58.6 us
  waiting for transfers between devices: 30.6 us -> 33.6 us
    all_gather x2 -> x1, blocking collectives: 29.1 us -> 16.7 us  [_shape_lots_all(): outer = lax.all_gather(part_next, ax_name, axis=0, tiled=True)]
    all_to_all x1, waiting for transfers between devices: 11.7 us -> 13.3 us  [body(): lax.all_to_all(m_x, 'ctx', split_axis=1, concat_axis=0, tiled=True)]
    unnamed x36 -> x39, local copies, waits for them, and re-layouts: 12 us -> 13 us
  transfers between devices with their start and end apart: 5 -> 5, of which waited for: 3 -> 3; matrix products, arithmetic and copies ran while one was open for 17% -> 18% of each run, Pallas kernels for 0% -> 0%
where the time goes in v1:
time: 149 us; the launch traced here: 148 us
  blocking collectives  58.6 us (39%)
  waiting for transfers between devices  33.6 us (23%)
  local copies, waits for them, and re-layouts  20.2 us (14%)
  starting transfers between devices  19.8 us (13%)
  matrix products  7.28 us (5%)
  other arithmetic  7.04 us (5%)
    all_gather x1, blocking collectives, _shape_lots_all(): outer = lax.all_gather(part_next, ax_name, axis=0, tiled=True)  16.7 us
    all_gather x1, blocking collectives, body(): lax.all_gather(m_b, 'ctx', axis=0, tiled=True)  14.2 us
    all_gather x1, blocking collectives, body(): lax.all_gather(m_c, 'ctx', axis=0, tiled=True)  13.9 us
    all_gather x1, blocking collectives, body(): lax.all_gather(dt_raw, 'ctx', axis=0, tiled=True)  13.7 us
    all_to_all x1, waiting for transfers between devices, body(): lax.all_to_all(m_x, 'ctx', split_axis=1, concat_axis=0, tiled=True)  13.3 us
    unnamed x39, local copies, waits for them, and re-layouts  13 us
    all_to_all x1, waiting for transfers between devices, body(): lax.all_to_all(m_z, 'ctx', split_axis=1, concat_axis=0, tiled=True)  12 us
    all_to_all x1, waiting for transfers between devices, body(): lax.all_to_all(gated, 'ctx', split_axis=0, concat_axis=1, tiled=True)  8.31 us
  transfers between devices with their start and end apart: 5, of which 3 were waited for; matrix products, arithmetic and copies ran while one was open for 18% of the time, Pallas kernels for 0%

profile of v1, /device:TPU:0, one launch (start us, length us, event | category | flops | bytes accessed | tf_op | source)
XLA Modules:
  0.0 147.7 jit_solution(5453998042836031995)
XLA Ops:
  0.7 1.0 copy.68
  1.7 1.0 copy.67
  2.6 16.7 %all_gather.12 = bf16[512,512]{0,1:T(8,128)(2,1)S(1)} all-gather(bf16[128,512]{0,1:T(8,128)(2,1)S(1)} %pad_maximum_fusion.6), channel_id=1, replica_groups=mesh['grp'=2,'ctx'=4,'hd'=4] {'ctx'}, dimensions={0}, use_global_device_ids=true | all-gather | bytes 655360 | tf_op jit(solution)/shard_map/all_gather | solution.py:17
  19.4 0.2 reshape.189
  19.6 0.1 broadcast_compare_fusion
  19.7 0.5 fusion.8
  20.3 0.5 fusion.9
  20.9 0.7 fusion.17
  21.6 0.9 copy.72
  22.4 3.7 %all-to-all-start = ((bf16[128,4,256]{2,0,1:T(8,128)(2,1)}), bf16[128,4,256]{2,0,1:T(8,128)(2,1)S(1)}, u32[]{:S(2)}, u32[]{:S(2)}) async-start(bf16[128,4,256]{2,0,1:T(8,128)(2,1)} %copy.72), calls=%async_computation | async-start | bytes 524288 | tf_op jit(solution)/shard_map/all_to_all | solution.py:161
  26.1 13.7 %all_gather.15 = bf16[512,32]{0,1:T(8,128)(2,1)S(1)} all-gather(bf16[128,32]{0,1:T(8,128)(2,1)S(1)} %copy-done.11), channel_id=1, replica_groups=mesh['grp'=2,'ctx'=4,'hd'=4] {'ctx'}, dimensions={0}, use_global_device_ids=true | all-gather | bytes 40960 | tf_op jit(solution)/shard_map/all_gather | solution.py:164
  39.8 0.1 reshape.199
  39.9 0.1 fusion.61
  40.2 0.1 reshape.200
  40.3 0.1 dynamic_slice.25
  40.4 0.1 compare_select_fusion
  40.5 0.1 copy.82
  40.6 0.1 dynamic_slice.26
  40.7 14.2 %all_gather.14 = bf16[512,256]{1,0:T(8,128)(2,1)S(1)} all-gather(bf16[128,256]{1,0:T(8,128)(2,1)S(1)} %copy-done.5), channel_id=1, replica_groups=mesh['grp'=2,'ctx'=4,'hd'=4] {'ctx'}, dimensions={0}, use_global_device_ids=true | all-gather | bytes 327680 | tf_op jit(solution)/shard_map/all_gather | solution.py:165
  55.0 13.9 %all_gather.13 = bf16[512,256]{1,0:T(8,128)(2,1)S(1)} all-gather(bf16[128,256]{1,0:T(8,128)(2,1)S(1)} %copy-done.6), channel_id=1, replica_groups=mesh['grp'=2,'ctx'=4,'hd'=4] {'ctx'}, dimensions={0}, use_global_device_ids=true | all-gather | bytes 327680 | tf_op jit(solution)/shard_map/all_gather | solution.py:166
  69.0 0.3 reduce_window_sum.11
  69.2 0.1 fusion.60
  69.3 0.7 copy.85
  70.1 0.7 copy.83
  70.8 1.0 copy.74
  71.8 1.0 copy.90
  72.8 0.1 copy.88
  72.9 0.1 dynamic_slice.27
  73.0 0.1 mul.218
  73.1 0.7 mul.219
  73.9 3.5 %all-to-all-start.2 = ((bf16[128,4,512]{0,2,1:T(8,128)(2,1)}), bf16[128,4,512]{0,2,1:T(8,128)(2,1)S(1)}, u32[]{:S(2)}, u32[]{:S(2)}) async-start(bf16[128,4,512]{0,2,1:T(8,128)(2,1)} %bitcast.18), calls=%async_computation.2 | async-start | bytes 1048576 | tf_op jit(solution)/shard_map/all_to_all | solution.py:159
  77.4 0.6 iota_compare_fusion
  78.0 0.9 fusion.62
  78.9 13.3 %all-to-all-done.2 = bf16[128,4,512]{0,2,1:T(8,128)(2,1)S(1)} async-done(((bf16[128,4,512]{0,2,1:T(8,128)(2,1)}), bf16[128,4,512]{0,2,1:T(8,128)(2,1)S(1)}, u32[]{:S(2)}, u32[]{:S(2)}) %all-to-all-start.2) | async-done | bytes 524320 | tf_op jit(solution)/shard_map/all_to_all | solution.py:159
  92.2 3.5 %all-to-all-start.3 = ((bf16[128,4,512]{0,2,1:T(8,128)(2,1)}), bf16[128,4,512]{0,2,1:T(8,128)(2,1)S(1)}, u32[]{:S(2)}, u32[]{:S(2)}) async-start(bf16[128,4,512]{0,2,1:T(8,128)(2,1)} %bitcast.46), calls=%async_computation.3 | async-start | bytes 1048576 | tf_op jit(solution)/shard_map/all_to_all | solution.py:160
  95.7 0.7 pad_maximum_fusion.3
  96.5 0.2 copy.75
  96.8 12.0 %all-to-all-done.3 = bf16[128,4,512]{0,2,1:T(8,128)(2,1)S(1)} async-done(((bf16[128,4,512]{0,2,1:T(8,128)(2,1)}), bf16[128,4,512]{0,2,1:T(8,128)(2,1)S(1)}, u32[]{:S(2)}, u32[]{:S(2)}) %all-to-all-start.3) | async-done | bytes 524320 | tf_op jit(solution)/shard_map/all_to_all | solution.py:160
  108.8 4.2 %all-to-all-start.1 = ((bf16[4,128,256]{2,1,0:T(8,128)(2,1)}), bf16[4,128,256]{2,1,0:T(8,128)(2,1)}, u32[]{:S(2)}, u32[]{:S(2)}) async-start(bf16[4,128,256]{2,1,0:T(8,128)(2,1)} %bitcast.15), calls=%async_computation.1 | async-start | bytes 524288 | tf_op jit(solution)/shard_map/all_to_all | solution.py:196
  113.0 0.2 copy.91
  113.3 0.9 pad_maximum_fusion
  114.2 0.5 reshape_reshape_reshape.3
  114.7 0.6 convert_multiply_fusion
  115.3 1.8 %fusion = f32[4,8,64,128]{3,2,1,0:T(8,128)S(1)} fusion(bf16[4,128,128,1]{2,1,3,0:T(8,128)(2,1)S(1)} %bitcast.143, f32[4,128,8,64]{3,2,1,0:T(8,128)S(1)} %convert_multiply_fusion), kind=kOutput, calls=%fused_computation.1 | convolution fusion | flops 402653184 | bytes 2228224 | tf_op jit(solution)/shard_map/vmap(jh,jhp,jn->hpn)/dot_general | solution.py:111
  117.1 0.1 slice_add_fusion
  117.2 0.1 fusion.58
  117.3 0.9 pad_add_fusion
  118.2 0.1 fusion.57
  118.3 0.2 pad.35
  118.5 6.2 %pad.65 = f32[4,8,64,128]{3,2,1,0:T(8,128)S(1)} pad(f32[2,8,64,128]{3,2,1,0:T(8,128)} %pad_add_fusion, f32[]{:T(128)} %constant.92.clone.1), padding=1_0_1x0_0_0x0_0_0x0_0_0 | pad | bytes 1572868
  124.8 0.1 slice_add_fusion.2
  124.9 0.8 copy-done.4
  125.7 2.7 %fusion.11 = f32[4,128,8,64]{1,3,2,0:T(8,128)S(1)} fusion(bf16[4,128,8,64]{3,2,1,0:T(8,128)(2,1)S(1)} %reshape_reshape_reshape.3, f32[4,128,8]{1,2,0:T(8,128)S(1)} %copy-done.7, f32[4,128,8]{1,2,0:T(8,128)S(1)} %copy-done.8, f32[4,128,128]{2,1,0:T(8,128)S(1)} %copy-done.4, pred[128,128]{1,0:T(8,128)(4,1)S(1)} %copy-done.9), kind=kOutput, calls=%fused_computation.14 | convolution fusion | flops 404750336 | bytes 1884160 | tf_op jit(solution)/shard_map/vmap(ijh,jhp->ihp)/dot_general | solution.py:109
  128.4 0.6 fusion.14
  129.1 0.3 copy.89
  129.5 1.2 fusion.36
  130.6 5.0 %all-to-all-start.4 = ((bf16[4,128,512]{2,1,0:T(8,128)(2,1)}), bf16[4,128,512]{2,1,0:T(8,128)(2,1)S(1)}, u32[]{:S(2)}, u32[]{:S(2)}) async-start(bf16[4,128,512]{2,1,0:T(8,128)(2,1)} %fusion.36), calls=%async_computation.4 | async-start | bytes 1048576 | tf_op jit(solution)/shard_map/all_to_all | solution.py:195
  135.6 1.1 copy.73
  136.8 0.9 copy.94
  137.6 8.3 %all-to-all-done.4 = bf16[4,128,512]{2,1,0:T(8,128)(2,1)S(1)} async-done(((bf16[4,128,512]{2,1,0:T(8,128)(2,1)}), bf16[4,128,512]{2,1,0:T(8,128)(2,1)S(1)}, u32[]{:S(2)}, u32[]{:S(2)}) %all-to-all-start.4) | async-done | bytes 524320 | tf_op jit(solution)/shard_map/all_to_all | solution.py:195
  145.9 0.3 copy.93
  146.2 0.2 bitcast_reduce_fusion
  146.4 0.3 fusion.19
  146.7 1.0 copy.95
  (67 shorter events, 0.8 us)
Async XLA Ops:
  0.6 18.8 %copy-start.3 = (bf16[128,1024]{1,0:T(8,128)(2,1)S(1)}, bf16[128,1024]{1,0:T(8,128)(2,1)}, u32[]{:S(2)}) copy-start(bf16[128,1024]{1,0:T(8,128)(2,1)} %param.12) | copy-start | bytes 786436
  20.8 5.2 %copy-start.11 = (bf16[128,32]{0,1:T(8,128)(2,1)S(1)}, bf16[128,32]{0,1:T(8,128)(2,1)}, u32[]{:S(2)}) copy-start(bf16[128,32]{0,1:T(8,128)(2,1)} %param.19) | copy-start | bytes 24580
  21.5 18.8 %copy-start.13 = (f32[32]{0:T(128)S(1)}, f32[32]{0:T(128)}, u32[]{:S(2)}) copy-start(f32[32]{0:T(128)} %param.20) | copy-start | bytes 388
  21.5 19.1 %copy-start.14 = (f32[32]{0:T(128)S(1)}, f32[32]{0:T(128)}, u32[]{:S(2)}) copy-start(f32[32]{0:T(128)} %param.21) | copy-start | bytes 388
  21.6 19.1 %copy-start.5 = (bf16[128,256]{1,0:T(8,128)(2,1)S(1)}, bf16[128,256]{1,0:T(8,128)(2,1)}, u32[]{:S(2)}) copy-start(bf16[128,256]{1,0:T(8,128)(2,1)} %param.17) | copy-start | bytes 196612
  21.6 33.4 %copy-start.6 = (bf16[128,256]{1,0:T(8,128)(2,1)S(1)}, bf16[128,256]{1,0:T(8,128)(2,1)}, u32[]{:S(2)}) copy-start(bf16[128,256]{1,0:T(8,128)(2,1)} %param.18) | copy-start | bytes 196612
  22.4 51.4 %all-to-all-start = ((bf16[128,4,256]{2,0,1:T(8,128)(2,1)}), bf16[128,4,256]{2,0,1:T(8,128)(2,1)S(1)}, u32[]{:S(2)}, u32[]{:S(2)}) async-start(bf16[128,4,256]{2,0,1:T(8,128)(2,1)} %copy.72), calls=%async_computation | async-start | bytes 524288 | tf_op jit(solution)/shard_map/all_to_all | solution.py:161
  54.9 15.9 %copy-start.1 = (bf16[128,2048]{1,0:T(8,128)(2,1)S(1)}, bf16[128,2048]{1,0:T(8,128)(2,1)}, u32[]{:S(2)}) copy-start(bf16[128,2048]{1,0:T(8,128)(2,1)} %param.15) | copy-start | bytes 1572868
  68.9 2.9 %copy-start.2 = (bf16[128,2048]{1,0:T(8,128)(2,1)S(1)}, bf16[128,2048]{1,0:T(8,128)(2,1)}, u32[]{:S(2)}) copy-start(bf16[128,2048]{1,0:T(8,128)(2,1)} %param.16) | copy-start | bytes 1572868
  69.2 3.7 %copy-start.15 = (f32[32]{0:T(128)S(1)}, f32[32]{0:T(128)}, u32[]{:S(2)}) copy-start(f32[32]{0:T(128)} %param.22) | copy-start | bytes 388
  73.9 18.4 %all-to-all-start.2 = ((bf16[128,4,512]{0,2,1:T(8,128)(2,1)}), bf16[128,4,512]{0,2,1:T(8,128)(2,1)S(1)}, u32[]{:S(2)}, u32[]{:S(2)}) async-start(bf16[128,4,512]{0,2,1:T(8,128)(2,1)} %bitcast.18), calls=%async_computation.2 | async-start | bytes 1048576 | tf_op jit(solution)/shard_map/all_to_all | solution.py:159
  92.2 16.5 %all-to-all-start.3 = ((bf16[128,4,512]{0,2,1:T(8,128)(2,1)}), bf16[128,4,512]{0,2,1:T(8,128)(2,1)S(1)}, u32[]{:S(2)}, u32[]{:S(2)}) async-start(bf16[128,4,512]{0,2,1:T(8,128)(2,1)} %bitcast.46), calls=%async_computation.3 | async-start | bytes 1048576 | tf_op jit(solution)/shard_map/all_to_all | solution.py:160
  108.8 21.9 %all-to-all-start.1 = ((bf16[4,128,256]{2,1,0:T(8,128)(2,1)}), bf16[4,128,256]{2,1,0:T(8,128)(2,1)}, u32[]{:S(2)}, u32[]{:S(2)}) async-start(bf16[4,128,256]{2,1,0:T(8,128)(2,1)} %bitcast.15), calls=%async_computation.1 | async-start | bytes 524288 | tf_op jit(solution)/shard_map/all_to_all | solution.py:196
  124.7 0.9 copy-start.4
  124.8 1.0 copy-start.7
  124.8 1.0 copy-start.8
  124.8 0.9 copy-start.9
  128.4 1.0 copy-start
  128.4 1.0 copy-start.12
  130.6 15.7 %copy-start.10 = (f32[2048]{0:T(1024)S(1)}, f32[2048]{0:T(1024)}, u32[]{:S(2)}) copy-start(f32[2048]{0:T(1024)} %param.23) | copy-start | bytes 24580
  130.6 15.3 %all-to-all-start.4 = ((bf16[4,128,512]{2,1,0:T(8,128)(2,1)}), bf16[4,128,512]{2,1,0:T(8,128)(2,1)S(1)}, u32[]{:S(2)}, u32[]{:S(2)}) async-start(bf16[4,128,512]{2,1,0:T(8,128)(2,1)} %fusion.36), calls=%async_computation.4 | async-start | bytes 1048576 | tf_op jit(solution)/shard_map/all_to_all | solution.py:195
